TPU v7x, 32 devices: a whole 2x2x4 slice. The times are simulated.
32 devices in a mesh: pipe: 4 (over y, core), vocab: 2 (over x), expert: 4 (over z).
Axes of the slice: x: 2, y: 2, z: 4, core: 2. Of those that a mesh axis runs over, the one named last changes fastest.
Arguments:
- token_ids: int32 [192], replicated, may hold values from 0 to 65535
- routes: int32 [192, 2], replicated, may hold values from 0 to 3, all different within a row; in each aligned block of 192 rows (0 to 191, 192 to 383, ...) at most 144 rows name the same one
- gate_weights: float32 [192, 2], replicated, may hold values from 0.2 to 1
- embed_table: bfloat16 [65536, 7168], P(('pipe', 'vocab'), 'expert'), may hold values from -0.59765625 to 0.59765625
- w_gate: bfloat16 [4, 7168, 2048], P('expert', None, ('pipe', 'vocab')), may hold values from -0.5 to 0.5
- w_up: bfloat16 [4, 7168, 2048], P('expert', None, ('pipe', 'vocab')), may hold values from -0.5 to 0.5
- w_down: bfloat16 [4, 2048, 7168], P('expert', ('pipe', 'vocab')), may hold values from -0.125 to 0.125
Outputs:
- logits: bfloat16 [192, 65536], P('expert', ('pipe', 'vocab'))
Inputs may be any that keep to these rules, and one draw needn't show every extreme that they name: `routes`: each row names 2 different experts; over all 192 rows no expert is named more than 144 times, a bound that some block reaches.
All inputs are finite; a program needn't handle non-finite values.
Results may differ from a plain program's by a relative error of at most 0.025.
Values may be sent and summed in bfloat16 or wider, within the bound.
A program may use at most 128 MiB of HBM per device.

v0:
```python
import jax
import jax.numpy as jnp
from jax import lax
from jax.sharding import PartitionSpec as P


def per_device(token_ids, routes, gate_weights, embed_table, w_gate, w_up, w_down):
    vocab_rows, width_cols = embed_table.shape
    tokens, top_count = routes.shape
    experts = lax.axis_size("expert")
    group_size = lax.axis_size(("pipe", "vocab"))
    capacity = group_size * (3 * tokens * top_count // (2 * experts * group_size))
    row_base = lax.axis_index(("pipe", "vocab")) * vocab_rows
    local_ids = token_ids - row_base
    in_shard = (local_ids >= 0) & (local_ids < vocab_rows)
    lookup_rows = jnp.take(embed_table, jnp.clip(local_ids, 0, vocab_rows - 1), axis=0)
    lookup_rows = jnp.where(in_shard[:, None], lookup_rows.astype(jnp.float32), 0.0)
    embedded = lax.psum(lookup_rows.astype(jnp.bfloat16), ("pipe", "vocab"))
    flat_routes = routes.reshape(-1)
    one_hot = (flat_routes[:, None] == jnp.arange(experts, dtype=jnp.int32)[None, :]).astype(
        jnp.int32
    )
    slot_index = jnp.sum((jnp.cumsum(one_hot, axis=0) - one_hot) * one_hot, axis=1)
    slot_dest = flat_routes * capacity + slot_index
    repeated = jnp.repeat(embedded, top_count, axis=0)
    buffer = jnp.zeros((experts * capacity, width_cols), jnp.bfloat16).at[slot_dest].set(repeated)
    buffer = buffer.reshape(experts, capacity, width_cols)
    flat_rows = lax.all_to_all(buffer, "expert", split_axis=0, concat_axis=2, tiled=True)[0]
    gate_proj = jnp.dot(flat_rows, w_gate[0], preferred_element_type=jnp.float32)
    up_proj = jnp.dot(flat_rows, w_up[0], preferred_element_type=jnp.float32)
    hidden = (jax.nn.silu(gate_proj) * up_proj).astype(jnp.bfloat16)
    partial_value = jnp.dot(hidden, w_down[0], preferred_element_type=jnp.float32)[None]
    shared = lax.psum_scatter(
        partial_value.astype(jnp.bfloat16), ("pipe", "vocab"), scatter_dimension=1, tiled=True
    ).astype(jnp.float32)
    shared = lax.all_to_all(
        shared.astype(jnp.bfloat16), "expert", split_axis=2, concat_axis=0, tiled=True
    ).astype(shared.dtype)
    returned = lax.all_gather(
        shared.astype(jnp.bfloat16), ("pipe", "vocab"), axis=1, tiled=True
    ).astype(shared.dtype)
    picked = returned.reshape(experts * capacity, width_cols)[slot_dest].reshape(
        tokens, top_count, width_cols
    )
    moe_out = jnp.sum(picked * gate_weights[:, :, None], axis=1)
    residual = (embedded.astype(jnp.float32) + moe_out).astype(jnp.bfloat16)
    return lax.psum_scatter(
        lax.dot_general(
            residual, embed_table, (((1,), (1,)), ((), ())), preferred_element_type=jnp.float32
        ).astype(jnp.bfloat16),
        "expert",
        scatter_dimension=0,
        tiled=True,
    )


def solution(mesh):
    return jax.shard_map(
        per_device,
        mesh=mesh,
        in_specs=(
            P(),
            P(),
            P(),
            P(("pipe", "vocab"), "expert"),
            P("expert", None, ("pipe", "vocab")),
            P("expert", None, ("pipe", "vocab")),
            P("expert", ("pipe", "vocab"), None),
        ),
        out_specs=P("expert", ("pipe", "vocab")),
        check_vma=False,
    )
```

profile of v0, /device:TPU:0, one launch (start us, length us, event | category | flops | bytes accessed | tf_op | source)
XLA Modules:
  0.0 428.2 jit_solution(8567750402209135640)
XLA Ops:
  6.5 0.0 all-reduce.4.cloned.1.call-start
  6.5 0.7 compare_and_fusion
  7.2 14.9 %gather_fusion = bf16[192,1792]{1,0:T(8,128)(2,1)S(1)} fusion(bf16[8192,1792]{1,0:T(8,128)(2,1)} %param.10, s32[1024]{0:T(1024)S(1)} %pad_clamp_fusion.1), kind=kCustom, calls=%fused_computation | custom fusion | bytes 1377024 | tf_op jit(solution)/shard_map/jit(_take)/gather | solution.py:16
  22.1 0.0 copy-start.2
  22.1 1.2 select_convert_fusion
  23.3 0.0 all-reduce.4.cloned.1.call-update
  23.3 0.0 all-gather.3.cloned.1.call-start
  23.4 0.0 copy-done.2
  23.4 0.1 copy.39
  23.5 0.1 eq.29
  23.7 0.1 eq.25
  23.8 1.2 reduce-window.6
  25.1 0.2 slice_reduce_fusion
  25.3 0.2 reduce-window.9
  25.5 0.1 copy.38
  25.6 0.1 mul.44
  25.7 0.1 add_bitcast_fusion
  25.9 55.8 %all-reduce.4.cloned.1.call-done = bf16[192,1792]{1,0:T(8,128)(2,1)} async-done(((bf16[192,1792]{1,0:T(8,128)(2,1)}), bf16[192,1792]{1,0:T(8,128)(2,1)}) %all-reduce.4.cloned.1.call-update) | async-done | bytes 688144 | tf_op jit(solution)/shard_map/psum | solution.py:18
  81.6 1.8 broadcast_in_dim.42
  83.4 0.6 reshape.98
  84.0 3.3 scatter_custom_fusion
  87.3 51.2 %all_to_all.33 = bf16[4,144,1792]{2,1,0:T(8,128)(2,1)S(1)} all-to-all(bf16[4,144,1792]{2,1,0:T(8,128)(2,1)S(1)} %bitcast.66), channel_id=1, replica_groups=mesh['pipe'=4,'vocab'=2,'expert'=4] {'expert'}, dimensions={0} | all-to-all | bytes 4128768 | tf_op jit(solution)/shard_map/all_to_all | solution.py:28
  138.5 1.1 copy.41
  139.5 0.0 copy-start
  139.6 0.3 copy.50
  139.8 1.8 copy-done
  141.6 0.8 fusion.5
  142.4 6.9 %fusion.1 = bf16[1,144,7168]{2,1,0:T(8,128)(2,1)} fusion(bf16[1,256,7168]{2,1,0:T(8,128)(2,1)} %param.13, bf16[144,7168]{1,0:T(8,128)(2,1)S(1)} %bitcast.63, bf16[1,7168,256]{2,1,0:T(8,128)(2,1)} %param.12, f32[144,256]{1,0:T(8,128)S(1)} %fusion.5), kind=kOutput, calls=%fused_computation.5 | convolution fusion | flops 1058217984 | bytes 11616256 | tf_op jit(solution)/shard_map/dot_general | solution.py:32
  149.2 0.0 copy-start.4
  149.2 58.3 %fusion = bf16[24,7168]{1,0:T(8,128)(2,1)S(1)} fusion(bf16[1,144,7168]{2,1,0:T(8,128)(2,1)} %fusion.1), kind=kCustom, calls=%all-reduce-scatter | all-reduce-scatter fusion | flops 1376257 | bytes 2408960
  207.6 1.9 collective-permute-start
  209.5 0.1 slice.13
  209.6 1.7 collective-permute-start.1
  211.3 0.0 copy-done.4
  211.3 0.6 dynamic-slice.4
  212.6 0.0 collective-permute-done.1
  212.6 4.5 %collective-permute-done = bf16[24,7168]{1,0:T(8,128)(2,1)S(1)} collective-permute-done((bf16[24,7168]{1,0:T(8,128)(2,1)S(1)}, bf16[24,7168]{1,0:T(8,128)(2,1)S(1)}, u32[]{:S(2)}, u32[]{:S(2)}) %collective-permute-start) | collective-permute-done | bytes 344096
  217.0 4.8 %concatenate = bf16[66,7168]{1,0:T(8,128)(2,1)S(1)} concatenate(bf16[18,7168]{1,0:T(8,128)(2,1)S(1)} %collective-permute-done.1, bf16[24,7168]{1,0:T(8,128)(2,1)S(1)} %collective-permute-done, bf16[24,7168]{1,0:T(8,128)(2,1)S(1)} %fusion), dimensions={0} | concatenate | bytes 1892352
  221.9 0.1 dynamic-slice_bitcast_fusion
  222.0 6.0 %copy.42 = bf16[1,18,7168]{1,0,2:T(2,128)(2,1)} copy(bf16[1,18,7168]{2,1,0:T(8,128)(2,1)S(1)} %dynamic-slice_bitcast_fusion) | data formatting | bytes 516096 | tf_op jit(solution)/shard_map/reduce_scatter | solution.py:33
  228.0 0.5 broadcast.68
  228.5 39.8 %reduce.4 = bf16[7168,18]{1,0:T(8,128)(2,1)S(1)} reduce(bf16[7168,1,18]{2,1,0:T(2,128)(2,1)} %bitcast.64, bf16[]{:T(256)} %broadcast.68), dimensions={1}, to_apply=%bitcast.56.reduce_sub_computation | reduce | bytes 516098
  268.3 3.4 reshape.114
  271.7 9.8 %all_to_all.34 = bf16[4,2,16128]{2,1,0:T(2,128)(2,1)S(1)} all-to-all(bf16[4,2,16128]{2,1,0:T(2,128)(2,1)S(1)} %reshape.114), channel_id=1, replica_groups=mesh['pipe'=4,'vocab'=2,'expert'=4] {'expert'}, dimensions={0} | all-to-all | bytes 516096 | tf_op jit(solution)/shard_map/all_to_all | solution.py:36
  281.4 5.2 %reshape.115 = bf16[7168,1,18]{2,1,0:T(2,128)(2,1)} reshape(bf16[4,2,16128]{2,1,0:T(2,128)(2,1)S(1)} %all_to_all.34) | data formatting | bytes 516096
  286.6 0.0 copy-start.3
  286.6 7.3 %copy.43 = bf16[1,18,7168]{2,1,0:T(8,128)(2,1)S(1)} copy(bf16[1,18,7168]{1,0,2:T(2,128)(2,1)} %bitcast.65) | data formatting | bytes 516096 | tf_op jit(solution)/shard_map/all_to_all | solution.py:36
  293.9 0.8 all_to_all.28
  294.7 0.0 all-gather.3.cloned.1.call-update
  294.7 0.3 reduce-scatter.5.cloned.1.call-start
  295.0 0.0 copy-done.3
  295.0 0.1 copy.46
  295.1 29.7 %all-gather.3.cloned.1.call-done = bf16[4,1,144,1792]{3,0,1,2:T(4,128)(2,1)} async-done(((bf16[4,1,18,1792]{3,0,1,2:T(4,128)(2,1)}), bf16[4,1,144,1792]{3,0,1,2:T(4,128)(2,1)}) %all-gather.3.cloned.1.call-update) | async-done | bytes 2064400 | tf_op jit(solution)/shard_map/all_gather | solution.py:39
  324.8 1.8 copy.45
  326.6 2.4 bitcast_convert_fusion
  329.0 6.1 %gather_fusion.1 = f32[384,1792]{1,0:T(8,128)S(1)} fusion(f32[576,1792]{1,0:T(8,128)} %bitcast_convert_fusion, s32[1024]{0:T(1024)S(1)} %pad_clamp_fusion), kind=kCustom, calls=%fused_computation.1 | custom fusion | bytes 5506560 | tf_op jit(solution)/shard_map/gather | solution.py:42
  335.1 2.8 reshape.75
  337.8 0.0 copy-start.1
  337.8 5.9 %multiply_reduce_fusion = f32[192,1792]{1,0:T(8,128)S(1)} fusion(f32[192,2,1792]{2,1,0:T(2,128)} %reshape.75, f32[192,2]{1,0:T(8,128)S(1)} %copy.46), kind=kLoop, calls=%fused_computation.11 | loop fusion | flops 1032192 | bytes 4130304 | tf_op jit(solution)/shard_map/reduce_sum | solution.py:45
  343.7 0.0 copy-done.1
  343.8 17.4 %convolution_convert_fusion = bf16[192,8192]{1,0:T(8,128)(2,1)} fusion(bf16[8192,1792]{1,0:T(8,128)(2,1)} %param.10, f32[192,1792]{1,0:T(8,128)S(1)} %multiply_reduce_fusion, bf16[192,1792]{1,0:T(8,128)(2,1)S(1)} %copy-done.1), kind=kOutput, calls=%fused_computation.3 | convolution fusion | flops 5639749632 | bytes 34570240 | tf_op jit(solution)/shard_map/dot_general | solution.py:48
  361.1 0.0 reduce-scatter.5.cloned.1.call-update
  361.1 60.6 %reduce-scatter.5.cloned.1.call-done = bf16[48,8192]{1,0:T(8,128)(2,1)} async-done(((bf16[192,8192]{1,0:T(8,128)(2,1)}), bf16[48,8192]{1,0:T(8,128)(2,1)}) %reduce-scatter.5.cloned.1.call-update) | async-done | bytes 786448 | tf_op jit(solution)/shard_map/reduce_scatter | solution.py:47
  (6 shorter events, 0.1 us)
Async XLA Ops:
  6.5 75.1 %all-reduce.4.cloned.1.call-start = ((), (), s32[]{:S(2)}) async-start(), calls=%async_computation.3 | async-start | bytes 1376256 | tf_op jit(solution)/shard_map/psum | solution.py:18
  22.1 1.3 copy-start.2
  23.3 301.5 %all-gather.3.cloned.1.call-start = ((), (), s32[]{:S(2)}) async-start(), calls=%async_computation.5 | async-start | bytes 2322432 | tf_op jit(solution)/shard_map/all_gather | solution.py:39
  139.5 2.0 copy-start
  149.2 62.1 %copy-start.4 = (u32[32]{0:T(128)S(1)}, u32[32]{0:T(128)}, u32[]{:S(2)}) copy-start(u32[32]{0:T(128)} %constant.54) | copy-start | bytes 388
  207.6 9.5 %collective-permute-start = (bf16[24,7168]{1,0:T(8,128)(2,1)S(1)}, bf16[24,7168]{1,0:T(8,128)(2,1)S(1)}, u32[]{:S(2)}, u32[]{:S(2)}) collective-permute-start(bf16[24,7168]{1,0:T(8,128)(2,1)S(1)} %fusion), channel_id=1, source_target_pairs={{0,4},{4,8},{8,12},{12,16},{16,20},{20,24},{24,28},{1,5},{5,9},{9,... | collective-permute-start | bytes 1032200
  209.6 3.0 collective-permute-start.1
  286.6 8.4 %copy-start.3 = (f32[192,2]{0,1:T(2,128)S(1)}, f32[192,2]{0,1:T(2,128)}, u32[]{:S(2)}) copy-start(f32[192,2]{0,1:T(2,128)} %param.9) | copy-start | bytes 4612
  294.7 127.0 %reduce-scatter.5.cloned.1.call-start = ((), (), s32[]{:S(2)}) async-start(), calls=%async_computation.4 | async-start | bytes 3932160 | tf_op jit(solution)/shard_map/reduce_scatter | solution.py:47
  337.8 5.9 %copy-start.1 = (bf16[192,1792]{1,0:T(8,128)(2,1)S(1)}, bf16[192,1792]{1,0:T(8,128)(2,1)}, u32[]{:S(2)}) copy-start(bf16[192,1792]{1,0:T(8,128)(2,1)} %all-reduce.4.cloned.1.call-done) | copy-start | bytes 2064388
Sparse Core Ops, SparseCore 0:
  23.5 58.1 all-reduce.3
  294.8 29.9 all-gather.2
  361.3 60.3 reduce-scatter.4
where the time goes:
time: 429 us; the launch traced here: 428 us
  waiting for transfers between devices  151 us (35%)
  blocking collectives  119 us (28%)
  local copies, waits for them, and re-layouts  64 us (15%)
  other arithmetic  51.5 us (12%)
  matrix products  25 us (6%)
  between operations  14 us (3%)
    reduce_scatter x1, waiting for transfers between devices, per_device(): lax.psum_scatter(lax.dot_general(residual, embed_table, (((1,), (1,)), ((...  60.6 us
    unnamed x1, blocking collectives  58.3 us
    psum x1, waiting for transfers between devices, per_device(): embedded = lax.psum(lookup_rows.astype(jnp.bfloat16), ('pipe', 'vocab'))  55.8 us
    all_to_all x1, blocking collectives, per_device(): lax.all_to_all(buffer, 'expert', split_axis=0, concat_axis=2, tiled=True)[0]  51.2 us
    unnamed x2, other arithmetic  39.8 us
    all_gather x1, waiting for transfers between devices, per_device(): lax.all_gather(shared.astype(jnp.bfloat16), ('pipe', 'vocab'), axis=1, ti...  29.7 us
    dot_general x1, matrix products, per_device(): lax.dot_general(residual, embed_table, (((1,), (1,)), ((), ())), preferre...  17.4 us
    unnamed x20, local copies, waits for them, and re-layouts  16.9 us
  transfers between devices with their start and end apart: 5, of which 4 were waited for; matrix products, arithmetic and copies ran while one was open for 1% of the time, Pallas kernels for 0%

commit v1 on v0

--- a/solution.py
+++ b/solution.py
@@ -2,6 +2,7 @@
 import jax.numpy as jnp
 from jax import lax
 from jax.sharding import PartitionSpec as P
+from jax.lax import psum
 
 
 def per_device(token_ids, routes, gate_weights, embed_table, w_gate, w_up, w_down):
@@ -15,7 +16,9 @@
     in_shard = (local_ids >= 0) & (local_ids < vocab_rows)
     lookup_rows = jnp.take(embed_table, jnp.clip(local_ids, 0, vocab_rows - 1), axis=0)
     lookup_rows = jnp.where(in_shard[:, None], lookup_rows.astype(jnp.float32), 0.0)
-    embedded = lax.psum(lookup_rows.astype(jnp.bfloat16), ("pipe", "vocab"))
+    embedded = lookup_rows.astype(jnp.bfloat16)
+    for ix in ("pipe", "vocab"):
+        embedded = psum(embedded, ix)
     flat_routes = routes.reshape(-1)
     one_hot = (flat_routes[:, None] == jnp.arange(experts, dtype=jnp.int32)[None, :]).astype(
         jnp.int32

time: 429 us -> 443 us (1.033)
  waiting for transfers between devices: 151 us -> 164 us
    psum x1 -> x2, waiting for transfers between devices: 55.8 us -> 69 us  [per_device(): embedded = psum(embedded, ix)]
  transfers between devices with their start and end apart: 5 -> 6, of which waited for: 4 -> 5; matrix products, arithmetic and copies ran while one was open for 1% -> 1% of each run, Pallas kernels for 0% -> 0%
where the time goes in v1:
time: 443 us
  waiting for transfers between devices  164 us (37%)
  blocking collectives  120 us (27%)
  local copies, waits for them, and re-layouts  64 us (14%)
  other arithmetic  51.5 us (12%)
  matrix products  25 us (6%)
  between operations  14 us (3%)
    psum x2, waiting for transfers between devices, per_device(): embedded = psum(embedded, ix)  69 us
    reduce_scatter x1, waiting for transfers between devices, per_device(): lax.psum_scatter(lax.dot_general(residual, embed_table, (((1,), (1,)), ((...  60.6 us
    unnamed x1, blocking collectives  58 us
    all_to_all x1, blocking collectives, per_device(): lax.all_to_all(buffer, 'expert', split_axis=0, concat_axis=2, tiled=True)[0]  51.7 us
    unnamed x2, other arithmetic  39.8 us
    all_gather x1, waiting for transfers between devices, per_device(): lax.all_gather(shared.astype(jnp.bfloat16), ('pipe', 'vocab'), axis=1, ti...  30.2 us
    dot_general x1, matrix products, per_device(): lax.dot_general(residual, embed_table, (((1,), (1,)), ((), ())), preferre...  17.3 us
    unnamed x20, local copies, waits for them, and re-layouts  16.9 us
  transfers between devices with their start and end apart: 6, of which 5 were waited for; matrix products, arithmetic and copies ran while one was open for 1% of the time, Pallas kernels for 0%

profile of v1, /device:TPU:0, one launch (start us, length us, event | category | flops | bytes accessed | tf_op | source)
XLA Modules:
  0.0 442.6 jit_solution(166587048812645597)
XLA Ops:
  6.5 0.0 all-reduce.5.cloned.1.call-start
  6.5 0.7 compare_and_fusion
  7.2 14.9 %gather_fusion = bf16[192,1792]{1,0:T(8,128)(2,1)S(1)} fusion(bf16[8192,1792]{1,0:T(8,128)(2,1)} %param.10, s32[1024]{0:T(1024)S(1)} %pad_clamp_fusion.1), kind=kCustom, calls=%fused_computation | custom fusion | bytes 1377024 | tf_op jit(solution)/shard_map/jit(_take)/gather | solution.py:17
  22.1 0.0 copy-start.2
  22.1 1.2 select_convert_fusion
  23.3 0.0 all-reduce.5.cloned.1.call-update
  23.3 0.0 all-reduce.7.cloned.1.call-start
  23.4 0.0 copy-done.2
  23.4 0.1 copy.39
  23.5 0.1 eq.29
  23.7 1.2 reduce-window.6
  24.9 35.5 %all-reduce.5.cloned.1.call-done = bf16[192,1792]{1,0:T(8,128)(2,1)} async-done(((bf16[192,1792]{1,0:T(8,128)(2,1)}), bf16[192,1792]{1,0:T(8,128)(2,1)}) %all-reduce.5.cloned.1.call-update) | async-done | bytes 688144 | tf_op jit(solution)/shard_map/psum | solution.py:21
  60.4 0.0 all-reduce.7.cloned.1.call-update
  60.4 0.0 all-gather.3.cloned.1.call-start
  60.5 0.2 slice_reduce_fusion
  60.7 0.1 eq.25
  60.8 0.2 reduce-window.9
  61.0 0.1 copy.38
  61.1 0.1 mul.44
  61.3 0.1 add_bitcast_fusion
  61.4 33.5 %all-reduce.7.cloned.1.call-done = bf16[192,1792]{1,0:T(8,128)(2,1)} async-done(((bf16[192,1792]{1,0:T(8,128)(2,1)}), bf16[192,1792]{1,0:T(8,128)(2,1)}) %all-reduce.7.cloned.1.call-update) | async-done | bytes 688144 | tf_op jit(solution)/shard_map/psum | solution.py:21
  95.0 1.8 broadcast_in_dim.42
  96.8 0.6 reshape.98
  97.3 3.3 scatter_custom_fusion
  100.6 51.7 %all_to_all.33 = bf16[4,144,1792]{2,1,0:T(8,128)(2,1)S(1)} all-to-all(bf16[4,144,1792]{2,1,0:T(8,128)(2,1)S(1)} %bitcast.66), channel_id=1, replica_groups=mesh['pipe'=4,'vocab'=2,'expert'=4] {'expert'}, dimensions={0} | all-to-all | bytes 4128768 | tf_op jit(solution)/shard_map/all_to_all | solution.py:31
  152.3 1.1 copy.41
  153.4 0.0 copy-start
  153.4 0.3 copy.50
  153.7 1.8 copy-done
  155.5 0.8 fusion.5
  156.3 6.9 %fusion.1 = bf16[1,144,7168]{2,1,0:T(8,128)(2,1)} fusion(bf16[1,256,7168]{2,1,0:T(8,128)(2,1)} %param.13, bf16[144,7168]{1,0:T(8,128)(2,1)S(1)} %bitcast.63, bf16[1,7168,256]{2,1,0:T(8,128)(2,1)} %param.12, f32[144,256]{1,0:T(8,128)S(1)} %fusion.5), kind=kOutput, calls=%fused_computation.5 | convolution fusion | flops 1058217984 | bytes 11616256 | tf_op jit(solution)/shard_map/dot_general | solution.py:35
  163.1 0.0 copy-start.4
  163.1 58.0 %fusion = bf16[24,7168]{1,0:T(8,128)(2,1)S(1)} fusion(bf16[1,144,7168]{2,1,0:T(8,128)(2,1)} %fusion.1), kind=kCustom, calls=%all-reduce-scatter | all-reduce-scatter fusion | flops 1376257 | bytes 2408960
  221.2 2.2 collective-permute-start
  223.4 0.1 slice.13
  223.5 1.7 collective-permute-start.1
  225.2 0.0 copy-done.4
  225.2 0.6 dynamic-slice.4
  226.5 0.0 collective-permute-done.1
  226.5 4.5 %collective-permute-done = bf16[24,7168]{1,0:T(8,128)(2,1)S(1)} collective-permute-done((bf16[24,7168]{1,0:T(8,128)(2,1)S(1)}, bf16[24,7168]{1,0:T(8,128)(2,1)S(1)}, u32[]{:S(2)}, u32[]{:S(2)}) %collective-permute-start) | collective-permute-done | bytes 344096
  230.9 4.8 %concatenate = bf16[66,7168]{1,0:T(8,128)(2,1)S(1)} concatenate(bf16[18,7168]{1,0:T(8,128)(2,1)S(1)} %collective-permute-done.1, bf16[24,7168]{1,0:T(8,128)(2,1)S(1)} %collective-permute-done, bf16[24,7168]{1,0:T(8,128)(2,1)S(1)} %fusion), dimensions={0} | concatenate | bytes 1892352
  235.8 0.1 dynamic-slice_bitcast_fusion
  235.9 6.0 %copy.42 = bf16[1,18,7168]{1,0,2:T(2,128)(2,1)} copy(bf16[1,18,7168]{2,1,0:T(8,128)(2,1)S(1)} %dynamic-slice_bitcast_fusion) | data formatting | bytes 516096 | tf_op jit(solution)/shard_map/reduce_scatter | solution.py:36
  241.9 0.5 broadcast.68
  242.4 39.8 %reduce.4 = bf16[7168,18]{1,0:T(8,128)(2,1)S(1)} reduce(bf16[7168,1,18]{2,1,0:T(2,128)(2,1)} %bitcast.64, bf16[]{:T(256)} %broadcast.68), dimensions={1}, to_apply=%bitcast.56.reduce_sub_computation | reduce | bytes 516098
  282.2 3.4 reshape.114
  285.6 9.7 %all_to_all.34 = bf16[4,2,16128]{2,1,0:T(2,128)(2,1)S(1)} all-to-all(bf16[4,2,16128]{2,1,0:T(2,128)(2,1)S(1)} %reshape.114), channel_id=1, replica_groups=mesh['pipe'=4,'vocab'=2,'expert'=4] {'expert'}, dimensions={0} | all-to-all | bytes 516096 | tf_op jit(solution)/shard_map/all_to_all | solution.py:39
  295.3 5.2 %reshape.115 = bf16[7168,1,18]{2,1,0:T(2,128)(2,1)} reshape(bf16[4,2,16128]{2,1,0:T(2,128)(2,1)S(1)} %all_to_all.34) | data formatting | bytes 516096
  300.5 7.3 %copy.43 = bf16[1,18,7168]{2,1,0:T(8,128)(2,1)S(1)} copy(bf16[1,18,7168]{1,0,2:T(2,128)(2,1)} %bitcast.65) | data formatting | bytes 516096 | tf_op jit(solution)/shard_map/all_to_all | solution.py:39
  307.8 0.8 all_to_all.28
  308.6 0.0 all-gather.3.cloned.1.call-update
  308.6 0.3 reduce-scatter.5.cloned.1.call-start
  308.9 0.0 copy-done.3
  308.9 0.1 copy.46
  309.0 30.2 %all-gather.3.cloned.1.call-done = bf16[4,1,144,1792]{3,0,1,2:T(4,128)(2,1)} async-done(((bf16[4,1,18,1792]{3,0,1,2:T(4,128)(2,1)}), bf16[4,1,144,1792]{3,0,1,2:T(4,128)(2,1)}) %all-gather.3.cloned.1.call-update) | async-done | bytes 2064400 | tf_op jit(solution)/shard_map/all_gather | solution.py:42
  339.2 1.8 copy.45
  341.0 2.4 bitcast_convert_fusion
  343.3 6.1 %gather_fusion.1 = f32[384,1792]{1,0:T(8,128)S(1)} fusion(f32[576,1792]{1,0:T(8,128)} %bitcast_convert_fusion, s32[1024]{0:T(1024)S(1)} %pad_clamp_fusion), kind=kCustom, calls=%fused_computation.1 | custom fusion | bytes 5506560 | tf_op jit(solution)/shard_map/gather | solution.py:45
  349.4 2.8 reshape.75
  352.2 5.9 %multiply_reduce_fusion = f32[192,1792]{1,0:T(8,128)S(1)} fusion(f32[192,2,1792]{2,1,0:T(2,128)} %reshape.75, f32[192,2]{1,0:T(8,128)S(1)} %copy.46), kind=kLoop, calls=%fused_computation.11 | loop fusion | flops 1032192 | bytes 4130304 | tf_op jit(solution)/shard_map/reduce_sum | solution.py:48
  358.1 0.0 copy-done.1
  358.1 17.3 %convolution_convert_fusion = bf16[192,8192]{1,0:T(8,128)(2,1)} fusion(bf16[8192,1792]{1,0:T(8,128)(2,1)} %param.10, f32[192,1792]{1,0:T(8,128)S(1)} %multiply_reduce_fusion, bf16[192,1792]{1,0:T(8,128)(2,1)S(1)} %copy-done.1), kind=kOutput, calls=%fused_computation.3 | convolution fusion | flops 5639749632 | bytes 34570240 | tf_op jit(solution)/shard_map/dot_general | solution.py:51
  375.5 0.0 reduce-scatter.5.cloned.1.call-update
  375.5 60.6 %reduce-scatter.5.cloned.1.call-done = bf16[48,8192]{1,0:T(8,128)(2,1)} async-done(((bf16[192,8192]{1,0:T(8,128)(2,1)}), bf16[48,8192]{1,0:T(8,128)(2,1)}) %reduce-scatter.5.cloned.1.call-update) | async-done | bytes 786448 | tf_op jit(solution)/shard_map/reduce_scatter | solution.py:50
  (8 shorter events, 0.1 us)
Async XLA Ops:
  6.5 53.9 %all-reduce.5.cloned.1.call-start = ((), (), s32[]{:S(2)}) async-start(), calls=%async_computation.3 | async-start | bytes 1376256 | tf_op jit(solution)/shard_map/psum | solution.py:21
  22.1 1.3 copy-start.2
  23.3 71.6 %all-reduce.7.cloned.1.call-start = ((), (), s32[]{:S(2)}) async-start(), calls=%async_computation.4 | async-start | bytes 1376256 | tf_op jit(solution)/shard_map/psum | solution.py:21
  60.4 278.8 %all-gather.3.cloned.1.call-start = ((), (), s32[]{:S(2)}) async-start(), calls=%async_computation.6 | async-start | bytes 2322432 | tf_op jit(solution)/shard_map/all_gather | solution.py:42
  153.4 2.0 copy-start
  163.1 62.1 %copy-start.4 = (u32[32]{0:T(128)S(1)}, u32[32]{0:T(128)}, u32[]{:S(2)}) copy-start(u32[32]{0:T(128)} %constant.54) | copy-start | bytes 388
  221.2 9.8 %collective-permute-start = (bf16[24,7168]{1,0:T(8,128)(2,1)S(1)}, bf16[24,7168]{1,0:T(8,128)(2,1)S(1)}, u32[]{:S(2)}, u32[]{:S(2)}) collective-permute-start(bf16[24,7168]{1,0:T(8,128)(2,1)S(1)} %fusion), channel_id=1, source_target_pairs={{0,4},{4,8},{8,12},{12,16},{16,20},{20,24},{24,28},{1,5},{5,9},{9,... | collective-permute-start | bytes 1032200
  223.5 3.0 collective-permute-start.1
  300.5 8.4 %copy-start.3 = (f32[192,2]{0,1:T(2,128)S(1)}, f32[192,2]{0,1:T(2,128)}, u32[]{:S(2)}) copy-start(f32[192,2]{0,1:T(2,128)} %param.9) | copy-start | bytes 4612
  308.6 127.4 %reduce-scatter.5.cloned.1.call-start = ((), (), s32[]{:S(2)}) async-start(), calls=%async_computation.5 | async-start | bytes 3932160 | tf_op jit(solution)/shard_map/reduce_scatter | solution.py:50
  352.2 5.9 %copy-start.1 = (bf16[192,1792]{1,0:T(8,128)(2,1)S(1)}, bf16[192,1792]{1,0:T(8,128)(2,1)}, u32[]{:S(2)}) copy-start(bf16[192,1792]{1,0:T(8,128)(2,1)} %all-reduce.7.cloned.1.call-done) | copy-start | bytes 2064388
Sparse Core Ops, SparseCore 0:
  23.5 36.8 all-reduce.4
  62.7 32.2 all-reduce.6
  308.7 30.4 all-gather.2
  375.6 60.3 reduce-scatter.4
